TPU v7x, 512 devices: a whole 4x4x16 slice. The times are simulated.
512 devices in a mesh: dp: 16 (over y, x), tensor: 32 (over z, core).
Axes of the slice: x: 4, y: 4, z: 16, core: 2. Of those that a mesh axis runs over, the one named last changes fastest.
Arguments:
- logits: bfloat16 [4096, 152064], P('dp', 'tensor'), may hold values from -120 to 256
- child_ids: int32 [4096, 64], P('dp'), may hold values from 0 to 152063
- leaf_counts: int32 [4096, 64], P('dp'), may hold values from 1 to 1024
- leaf_valid: int32 [4096], P('dp'), may hold values from 1 to 64
- leaf_temp: float32 [4096], P('dp'), may hold values from 0.5 to 2
- leaf_owner: int32 [4096], P('dp'), may hold values from 0 to 4095, as said below
Outputs:
- gradient: bfloat16 [4096, 152064], P('dp', 'tensor')
- row_loss: float32 [4096], P('dp')
- mean_loss: float32 [], replicated
Inputs may be any that keep to these rules, and one draw needn't show every extreme that they name: `leaf_owner`: every position is named by exactly one leaf row. Of the leaf rows of one dp index, exactly 16 name positions of each owner index.
All inputs are finite; a program needn't handle non-finite values.
Results may differ from a plain program's by a relative error of at most 0.001.
Values may be sent and summed in bfloat16 or wider, within the bound.
A program may use at most 64 MiB of HBM per device.

v0:
```python
import jax
import jax.numpy as jnp
from jax import lax
from jax.sharding import PartitionSpec as P


def sent_to_all(value, axis):
    count = lax.axis_size(axis)
    return lax.all_to_all(
        jnp.broadcast_to(value[None], (count, *value.shape)), axis, 0, 0, tiled=True
    )


def all_in_one(value, axis):
    leaves = jax.tree.leaves(value)
    order = sorted(range(len(leaves)), key=lambda k: -leaves[k].size)
    width = (1, *leaves[order[0]].shape)[-1]
    lines = [
        jnp.pad(leaves[k].reshape(-1), (0, -leaves[k].size % width)).reshape(-1, width)
        for k in order
    ]
    both, at, found = (sent_to_all(jnp.concatenate(lines), axis), 0, {})
    for k, line in zip(order, lines):
        share = both[:, at : at + len(line)].reshape(len(both), -1)
        found[k] = share[:, : leaves[k].size].reshape(-1, *leaves[k].shape)
        at += len(line)
    numbers = iter(range(len(leaves)))
    return jax.tree.map(lambda _: found[next(numbers)], value)


def joined_by_halves(pieces, combine):
    while len(jax.tree.leaves(pieces)[0]) > 1:
        pieces = jax.vmap(combine)(
            *(jax.tree.map(lambda part: part[side::2], pieces) for side in (0, 1))
        )
    return jax.tree.map(lambda part: part[0], pieces)


def combined_all(value, axis, combine):
    pieces = all_in_one(value, axis)
    return joined_by_halves(pieces, combine)


def over_copies(value, axis):
    return sent_to_all(value, axis).sum(axis=0)


def combine_stats(earlier, later):
    top_first, sum_first, picked_first = earlier
    top_second, sum_second, picked_second = later
    row_top = jnp.maximum(top_first, top_second)
    sumexp = sum_first * jnp.exp(top_first - row_top) + sum_second * jnp.exp(top_second - row_top)
    return (row_top, sumexp, picked_first + picked_second)


def select_rows(matcher, values):
    return jnp.dot(
        matcher, values, preferred_element_type=jnp.float32, precision=lax.Precision.HIGHEST
    )


def body(logits, child_ids, leaf_counts, leaf_valid, leaf_temp, leaf_owner):
    pos_dev = logits.shape[0]
    columns_dev = logits.shape[1]
    children = leaf_counts.shape[1]
    groups = lax.axis_size("dp")
    slot_index = jnp.arange(children, dtype=jnp.int32)
    in_use = slot_index[None, :] < leaf_valid[:, None]
    powered = jnp.exp(jnp.log(leaf_counts.astype(jnp.float32)) * leaf_temp[:, None])
    weights = jnp.where(in_use, powered, jnp.float32(0.0))
    owner_dev = leaf_owner // pos_dev
    local_slot = leaf_owner % pos_dev
    onehot = (owner_dev[:, None] == jnp.arange(groups, dtype=jnp.int32)[None, :]).astype(jnp.int32)
    slot_rank = jnp.sum((jnp.cumsum(onehot, axis=0) - onehot) * onehot, axis=1)
    capacity = pos_dev // groups
    destination = owner_dev * capacity + slot_rank
    send_index = jnp.arange(groups * capacity, dtype=jnp.int32)
    sender = send_index[:, None] == destination[None, :]
    outgoing = select_rows(sender.astype(jnp.float32), weights).reshape(groups, capacity, children)
    labels = jnp.sum(jnp.where(sender, local_slot[None, :], 0), axis=1).reshape(groups, capacity)
    incoming, incoming_labels = (
        lax.all_to_all(outgoing, "dp", split_axis=0, concat_axis=0, tiled=True),
        lax.all_to_all(labels, "dp", split_axis=0, concat_axis=0, tiled=True),
    )
    receive_slot = incoming_labels.reshape(-1)
    receiver = (jnp.arange(pos_dev, dtype=jnp.int32)[:, None] == receive_slot[None, :]).astype(
        jnp.float32
    )
    placed = select_rows(receiver, incoming.reshape(-1, children))
    targets = placed / jnp.sum(placed, axis=1)[:, None]
    column_start = lax.axis_index("tensor") * columns_dev
    local_ids = child_ids - column_start
    column_index = jnp.arange(columns_dev, dtype=jnp.int32)
    matches = local_ids[:, None, :] == column_index[None, :, None]
    target_dense = jnp.sum(jnp.where(matches, targets[:, None, :], jnp.float32(0.0)), axis=2)
    values = logits.astype(jnp.float32)
    picked_part = jnp.sum(target_dense * values, axis=1)
    own_top_narrow = jnp.max(logits, axis=1)
    own_top = own_top_narrow.astype(jnp.float32)
    own_sum = jnp.sum(jnp.exp(values - own_top[:, None]), axis=1)
    row_top, sumexp, picked = combined_all((own_top, own_sum, picked_part), "tensor", combine_stats)
    row_loss = row_top + jnp.log(sumexp) - picked
    scale = 1.0 / sumexp
    gradient = (jnp.exp(values - row_top[:, None]) * scale[:, None] - target_dense).astype(
        jnp.bfloat16
    )
    loss_sum = over_copies(jnp.sum(row_loss), "dp")
    mean_loss = loss_sum / (groups * pos_dev)
    return (gradient, row_loss, mean_loss)


def solution(mesh):
    return jax.shard_map(
        body,
        mesh=mesh,
        in_specs=(P("dp", "tensor"), P("dp", None), P("dp", None), P("dp"), P("dp"), P("dp")),
        out_specs=(P("dp", "tensor"), P("dp"), P()),
        check_vma=False,
    )
```

profile of v0, /device:TPU:1, one launch (start us, length us, event | category | flops | bytes accessed | tf_op | source)
XLA Modules:
  0.0 133.3 jit_solution(3746079995882126552)
XLA Ops:
  0.6 0.0 copy-start.1
  0.6 0.8 and_select_fusion
  1.5 0.6 reduce-window.6
  2.1 0.2 slice_reduce_fusion
  2.3 0.1 fusion.21
  2.4 0.1 select_reduce_fusion.1
  2.5 0.7 all_to_all.16
  3.2 7.6 %all-to-all-start = ((s32[16,1,16]{2,1,0:T(1,128)}), s32[16,1,16]{2,1,0:T(1,128)S(1)}, u32[]{:S(2)}, u32[]{:S(2)}) async-start(s32[16,1,16]{2,1,0:T(1,128)} %all_to_all.16), calls=%async_computation | async-start | bytes 16384 | tf_op jit(solution)/shard_map/all_to_all | solution.py:83
  10.8 1.1 fusion.7
  11.9 0.8 reshape.101
  12.7 4.5 %all-to-all-done = s32[16,1,16]{2,1,0:T(1,128)S(1)} async-done(((s32[16,1,16]{2,1,0:T(1,128)}), s32[16,1,16]{2,1,0:T(1,128)S(1)}, u32[]{:S(2)}, u32[]{:S(2)}) %all-to-all-start) | async-done | bytes 1056 | tf_op jit(solution)/shard_map/all_to_all | solution.py:83
  17.2 3.5 %all-to-all-start.1 = ((f32[16,1,1024]{2,1,0:T(1,128)}), f32[16,1,1024]{2,1,0:T(1,128)S(1)}, u32[]{:S(2)}, u32[]{:S(2)}) async-start(f32[16,1,1024]{2,1,0:T(1,128)} %reshape.101), calls=%async_computation.1 | async-start | bytes 131072 | tf_op jit(solution)/shard_map/all_to_all | solution.py:82
  20.7 0.9 broadcast_subtract_fusion
  21.6 2.3 %reduce_max.9 = bf16[256]{0:T(256)(128)(2,1)S(1)} reduce(bf16[256,4752]{0,1:T(8,128)(2,1)} %param.6, bf16[]{:T(256)} %constant.37.clone.1), dimensions={1}, to_apply=%region_0.1 | reduce | flops 1216256 | bytes 2433538 | tf_op jit(solution)/shard_map/reduce_max | solution.py:98
  23.9 0.5 broadcast.72
  24.5 0.7 reduce.6
  25.1 0.1 eq.80
  25.2 2.0 %all-to-all-done.1 = f32[16,1,1024]{2,1,0:T(1,128)S(1)} async-done(((f32[16,1,1024]{2,1,0:T(1,128)}), f32[16,1,1024]{2,1,0:T(1,128)S(1)}, u32[]{:S(2)}, u32[]{:S(2)}) %all-to-all-start.1) | async-done | bytes 65568 | tf_op jit(solution)/shard_map/all_to_all | solution.py:82
  27.2 0.5 broadcast.74
  27.7 0.8 reduce.7
  28.5 0.1 reshape.102
  28.6 0.3 fusion.29
  28.9 51.1 %select_reduce_fusion = f32[256,4752]{0,1:T(8,128)S(1)} fusion(f32[256,64]{0,1:T(8,128)S(1)} %broadcast_divide_fusion, s32[256,64]{0,1:T(8,128)S(1)} %broadcast_subtract_fusion), kind=kLoop, calls=%fused_computation | loop fusion | flops 232353792 | bytes 4997120 | tf_op jit(solution)/shard_map/reduce_sum | solution.py:95
  80.1 0.0 copy-start
  80.1 2.2 %copy-done = f32[256,4752]{0,1:T(8,128)} copy-done((f32[256,4752]{0,1:T(8,128)}, f32[256,4752]{0,1:T(8,128)S(1)}, u32[]{:S(2)}) %copy-start) | copy-done | bytes 4866072
  82.2 0.0 copy-done.1
  82.2 1.4 %fusion.1 = (f32[256]{0:T(256)S(1)}, f32[256]{0:T(256)S(1)}) fusion(bf16[256,4752]{0,1:T(8,128)(2,1)S(1)} %copy-done.1, f32[256]{0:T(256)S(1)} %convert_element_type.45, f32[256,4752]{0,1:T(8,128)S(1)} %select_reduce_fusion), kind=kLoop, calls=%fused_computation.6 | loop fusion | flops 6082048 | bytes 7302144 | tf_op jit(solution)/shard_map/reduce_sum | solution.py:100
  83.6 34.0 %all_to_all.25 = f32[32,3,256]{2,1,0:T(4,128)S(1)} all-to-all(f32[32,3,256]{2,1,0:T(4,128)S(1)} %broadcast_in_dim.37), channel_id=1, replica_groups=mesh['dp'=16,'tensor'=32] {'tensor'}, dimensions={0} | all-to-all | bytes 196608 | tf_op jit(solution)/shard_map/all_to_all | solution.py:9
  117.6 0.1 fusion.28
  118.4 1.2 fusion.25
  119.5 1.2 broadcast_in_dim.38
  120.8 3.7 %all-to-all-start.3 = ((f32[16,1,1]{2,1,0:T(1,128)}), f32[16,1,1]{2,1,0:T(1,128)S(1)}, u32[]{:S(2)}, u32[]{:S(2)}) async-start(f32[16,1,1]{2,1,0:T(1,128)} %broadcast_in_dim.38), calls=%async_computation.3 | async-start | bytes 16384 | tf_op jit(solution)/shard_map/all_to_all | solution.py:9
  124.5 4.8 %fusion.6 = bf16[256,4752]{0,1:T(8,128)(2,1)} fusion(f32[256,4752]{0,1:T(8,128)} %copy-done, bf16[256,4752]{0,1:T(8,128)(2,1)S(1)} %copy-done.1, f32[256]{0:T(256)S(1)} %bitcast.49, f32[256]{0:T(256)S(1)} %bitcast.43), kind=kLoop, calls=%fused_computation.11 | loop fusion | flops 6082560 | bytes 9734144 | tf_op jit(solution)/shard_map/convert_element_type | solution.py:104
  129.3 1.6 %all-to-all-done.3 = f32[16,1,1]{2,1,0:T(1,128)S(1)} async-done(((f32[16,1,1]{2,1,0:T(1,128)}), f32[16,1,1]{2,1,0:T(1,128)S(1)}, u32[]{:S(2)}, u32[]{:S(2)}) %all-to-all-start.3) | async-done | bytes 96 | tf_op jit(solution)/shard_map/all_to_all | solution.py:9
  130.9 0.6 reduce_sum.79
  (45 shorter events, 0.7 us)
Async XLA Ops:
  0.6 81.6 %copy-start.1 = (bf16[256,4752]{0,1:T(8,128)(2,1)S(1)}, bf16[256,4752]{0,1:T(8,128)(2,1)}, u32[]{:S(2)}) copy-start(bf16[256,4752]{0,1:T(8,128)(2,1)} %param.6) | copy-start | bytes 7299076
  3.2 14.0 %all-to-all-start = ((s32[16,1,16]{2,1,0:T(1,128)}), s32[16,1,16]{2,1,0:T(1,128)S(1)}, u32[]{:S(2)}, u32[]{:S(2)}) async-start(s32[16,1,16]{2,1,0:T(1,128)} %all_to_all.16), calls=%async_computation | async-start | bytes 16384 | tf_op jit(solution)/shard_map/all_to_all | solution.py:83
  17.2 10.0 %all-to-all-start.1 = ((f32[16,1,1024]{2,1,0:T(1,128)}), f32[16,1,1024]{2,1,0:T(1,128)S(1)}, u32[]{:S(2)}, u32[]{:S(2)}) async-start(f32[16,1,1024]{2,1,0:T(1,128)} %reshape.101), calls=%async_computation.1 | async-start | bytes 131072 | tf_op jit(solution)/shard_map/all_to_all | solution.py:82
  80.1 2.2 %copy-start = (f32[256,4752]{0,1:T(8,128)}, f32[256,4752]{0,1:T(8,128)S(1)}, u32[]{:S(2)}) copy-start(f32[256,4752]{0,1:T(8,128)S(1)} %select_reduce_fusion) | copy-start | bytes 14598148
  120.8 10.2 %all-to-all-start.3 = ((f32[16,1,1]{2,1,0:T(1,128)}), f32[16,1,1]{2,1,0:T(1,128)S(1)}, u32[]{:S(2)}, u32[]{:S(2)}) async-start(f32[16,1,1]{2,1,0:T(1,128)} %broadcast_in_dim.38), calls=%async_computation.3 | async-start | bytes 16384 | tf_op jit(solution)/shard_map/all_to_all | solution.py:9
where the time goes:
time: 134 us; the launch traced here: 133 us
  other arithmetic  65.6 us (49%)
  blocking collectives  34 us (25%)
  starting transfers between devices  14.8 us (11%)
  waiting for transfers between devices  8.12 us (6%)
  local copies, waits for them, and re-layouts  6.81 us (5%)
  between operations  2.56 us (2%)
  matrix products  1.43 us (1%)
    reduce_sum x1, other arithmetic, body(): jnp.sum(jnp.where(matches, targets[:, None, :], jnp.float32(0.0)), axis=2)  51.1 us
    all_to_all x1, blocking collectives, sent_to_all(): lax.all_to_all(jnp.broadcast_to(value[None], (count, *value.shape)), axis...  34 us
    all_to_all x1, starting transfers between devices, body(): lax.all_to_all(labels, 'dp', split_axis=0, concat_axis=0, tiled=True)  7.57 us
    convert_element_type x1, other arithmetic, body(): (jnp.exp(values - row_top[:, None]) * scale[:, None] - target_dense).asty...  4.84 us
    all_to_all x1, waiting for transfers between devices, body(): lax.all_to_all(labels, 'dp', split_axis=0, concat_axis=0, tiled=True)  4.53 us
    all_to_all x1, starting transfers between devices, sent_to_all(): lax.all_to_all(jnp.broadcast_to(value[None], (count, *value.shape)), axis...  3.73 us
    all_to_all x1, starting transfers between devices, body(): lax.all_to_all(outgoing, 'dp', split_axis=0, concat_axis=0, tiled=True)  3.5 us
    unnamed x7, local copies, waits for them, and re-layouts  3.03 us
  transfers between devices with their start and end apart: 3, of which 3 were waited for; matrix products, arithmetic and copies ran while one was open for 8% of the time, Pallas kernels for 0%

commit v1 on v0

v1 whole, which is shorter than its diff:
```python
import functools

import jax
import jax.numpy as jnp
from jax import lax
from jax.experimental import pallas as pl
from jax.experimental.pallas import tpu as pltpu
from jax.sharding import PartitionSpec as P

MESH = pl.DeviceIdType.MESH
F32 = jnp.float32
BF16 = jnp.bfloat16
LANES = 128
WIDE = 256
CHUNK = 176


def dot_nt(lhs, rhs):
    return lax.dot_general(lhs, rhs, (((1,), (1,)), ((), ())), preferred_element_type=F32)


def split(value):
    high = value.astype(BF16)
    rest = value - high.astype(F32)
    middle = rest.astype(BF16)
    return high, middle, (rest - middle.astype(F32)).astype(BF16)


def iota(shape, dim):
    return lax.broadcasted_iota(jnp.int32, shape, dim)


def kernel(
    groups, shards,
    x_hbm, ids_ref, count_ref, valid_ref, temp_ref, owner_ref,
    grad_hbm, loss_ref, mean_ref,
    xs, es, dense, spread, gout, outbuf, inbuf, placed, ids_rows,
    stat_send, stat_buf, pick_send, pick_buf, mean_send, mean_buf,
    x_sem, grad_sem, send_sem, route_sem, stat_sem, pick_sem, mean_sem,
):
    cols, pos = x_hbm.shape
    child = ids_ref.shape[0]
    cap = pos // groups
    my_dp = lax.axis_index("dp")
    my_t = lax.axis_index("tensor")
    heads = pl.cdiv(cols, WIDE)

    x_copy = pltpu.make_async_copy(x_hbm, xs, x_sem)
    x_copy.start()

    barrier = pltpu.get_barrier_semaphore()

    def greet_dp(k, _):
        pl.semaphore_signal(barrier, inc=1, device_id={"dp": lax.rem(my_dp + k, groups)}, device_id_type=MESH)
        return 0

    def greet_t(k, _):
        pl.semaphore_signal(barrier, inc=1, device_id={"tensor": lax.rem(my_t + k, shards)}, device_id_type=MESH)
        return 0

    lax.fori_loop(1, groups, greet_dp, 0)
    lax.fori_loop(1, shards, greet_t, 0)

    powered = jnp.exp(jnp.log(count_ref[...].astype(F32)) * temp_ref[...])
    weights = jnp.where(iota((child, pos), 0) < valid_ref[...], powered, 0.0)
    share = weights / jnp.sum(weights, axis=0, keepdims=True)
    owner = owner_ref[...]
    shift = pos.bit_length() - 1
    owner_dp = lax.shift_right_logical(owner, shift)
    place = lax.bitwise_and(owner, pos - 1)
    member = jnp.where(iota((groups, pos), 0) == owner_dp, 1.0, 0.0).astype(F32)
    before = jnp.where(iota((pos, pos), 0) < iota((pos, pos), 1), 1.0, 0.0).astype(BF16)
    earlier = jnp.dot(member.astype(BF16), before, preferred_element_type=F32)
    rank = jnp.sum(member * earlier, axis=0, keepdims=True)
    target_row = owner_dp * cap + rank.astype(jnp.int32)
    sender = jnp.where(iota((pos, pos), 0) == target_row, 1.0, 0.0).astype(BF16)
    high, middle, low = split(share)
    place_rows = jnp.broadcast_to(place.astype(F32), (child, pos)).astype(BF16)
    none = jnp.zeros_like(low)
    outgoing = dot_nt(sender, jnp.concatenate([high, place_rows], axis=0))
    outgoing = outgoing + dot_nt(sender, jnp.concatenate([middle, none], axis=0))
    outgoing = outgoing + dot_nt(sender, jnp.concatenate([low, none], axis=0))
    outbuf[...] = outgoing.reshape(groups, cap, 2 * child)

    local = ids_ref[...] - my_t * cols
    ids_rows[...] = jnp.transpose(jnp.concatenate([local, local], axis=0))

    x_copy.wait()
    steps = cols // CHUNK

    def part(g):
        return pl.ds(pl.multiple_of(g * CHUNK, CHUNK), CHUNK)

    def fold(value):
        return value.reshape(CHUNK // 8, 8, pos)

    def tops(g, top):
        return jnp.maximum(top, jnp.max(fold(xs[part(g), :].astype(F32)), axis=0))

    top = lax.fori_loop(1, steps, tops, jnp.max(fold(xs[0:CHUNK, :].astype(F32)), axis=0))
    top = jnp.max(top, axis=0, keepdims=True)

    def sums(g, total):
        powers = jnp.exp(xs[part(g), :].astype(F32) - top)
        es[part(g), :] = powers
        return total + jnp.sum(fold(powers), axis=0)

    total = lax.fori_loop(0, steps, sums, jnp.zeros((8, pos), F32))
    own_stats = jnp.concatenate([top, jnp.sum(total, axis=0, keepdims=True)], axis=0)
    stat_send[...] = own_stats
    stat_buf[pl.ds(my_t, 1)] = own_stats.reshape(1, 2, pos)

    pl.semaphore_wait(barrier, groups - 1 + shards - 1)

    def route(k, _):
        peer = lax.rem(my_dp + k, groups)
        pltpu.make_async_remote_copy(
            outbuf.at[peer], inbuf.at[my_dp], send_sem.at[0], route_sem,
            device_id={"dp": peer}, device_id_type=MESH,
        ).start()
        return 0

    def cast(source, buffer, slot, sem, axis, me, count):
        def one(k, _):
            pltpu.make_async_remote_copy(
                source, buffer.at[me], send_sem.at[slot], sem,
                device_id={axis: lax.rem(me + k, count)}, device_id_type=MESH,
            ).start()
            return 0

        lax.fori_loop(1, count, one, 0)

    def take(buffer, count, sem):
        piece = buffer.at[pl.ds(0, count)]
        pltpu.make_async_copy(piece, piece, sem).wait()

    lax.fori_loop(1, groups, route, 0)
    cast(stat_send, stat_buf, 1, stat_sem, "tensor", my_t, shards)
    inbuf[pl.ds(my_dp, 1)] = outbuf[pl.ds(my_dp, 1)]

    take(inbuf, groups - 1, route_sem)
    turned = jnp.transpose(inbuf[...].reshape(pos, 2 * child))
    high, middle, low = split(turned[:child])
    label = turned[child : child + 1].astype(jnp.int32)
    receiver = jnp.where(iota((pos, pos), 0) == label, 1.0, 0.0).astype(BF16)
    placed[...] = dot_nt(receiver, jnp.concatenate([high, middle, low, low], axis=0))

    block = 8
    width = block * child
    lane = iota((block, LANES), 1)
    half = (lane >= child).astype(jnp.int32)
    row8 = iota((block, LANES), 0)
    per = LANES // child
    pieces = width // LANES
    spread_rows = iota((WIDE, width), 0)

    def target_rows(g, _):
        rows = pl.ds(pl.multiple_of(g * block, block), block)
        local = ids_rows[rows, :]
        head = lax.shift_right_arithmetic(local, 8)
        rest = lax.bitwise_and(local, WIDE - 1)
        parts = placed[rows, 0:LANES]
        swapped = pltpu.roll(parts, child, 1)
        high2 = jnp.where(lane < child, parts, swapped)
        middle2 = jnp.where(lane < child, swapped, parts)
        low2 = placed[rows, LANES : 2 * LANES]
        heads_at, rests_at = [], []
        for c in range(pieces):
            own = row8 == per * c + half
            heads_at.append(jnp.where(own, head, -1))
            rests_at.append(jnp.sum(jnp.where(own, rest, 0), axis=0, keepdims=True))
        onehot = jnp.where(spread_rows == jnp.concatenate(rests_at, axis=1), 1.0, 0.0).astype(BF16)
        hits = [[at == h for at in heads_at] for h in range(heads)]
        found = jnp.zeros((heads * block, WIDE), F32)
        for value in (high2, middle2, low2):
            chosen = [jnp.concatenate([jnp.where(at, value, 0.0) for at in hit], axis=1) for hit in hits]
            found = found + dot_nt(jnp.concatenate(chosen, axis=0).astype(BF16), onehot)
        for h in range(heads):
            dense[rows, h * WIDE : (h + 1) * WIDE] = found[h * block : (h + 1) * block]
        return 0

    lax.fori_loop(0, pos // block, target_rows, 0)

    def turn(b, total):
        at = pl.multiple_of(b * LANES, LANES)
        tile = jnp.transpose(dense[:, pl.ds(at, LANES)])
        spread[pl.ds(at, LANES), :] = tile
        product = tile * xs[pl.ds(at, LANES), :].astype(F32)
        return total + jnp.sum(product.reshape(LANES // 8, 8, pos), axis=0)

    whole = cols // LANES
    total = lax.fori_loop(0, whole, turn, jnp.zeros((8, pos), F32))
    left = cols - whole * LANES
    if left:
        tile = jnp.transpose(dense[:, whole * LANES : (whole + 1) * LANES])[:left]
        spread[whole * LANES : cols, :] = tile
        product = tile * xs[whole * LANES : cols, :].astype(F32)
        total = total + jnp.sum(product.reshape(left // 8, 8, pos), axis=0)
    own_pick = jnp.sum(total, axis=0, keepdims=True)
    pick_send[...] = own_pick
    pick_buf[pl.ds(my_t, 1)] = own_pick.reshape(1, 1, pos)
    cast(pick_send, pick_buf, 2, pick_sem, "tensor", my_t, shards)

    take(stat_buf, shards - 1, stat_sem)
    every_top, every_sum = stat_buf[:, 0, :], stat_buf[:, 1, :]
    peak = jnp.max(every_top, axis=0, keepdims=True)
    whole_sum = jnp.sum(every_sum * jnp.exp(every_top - peak), axis=0, keepdims=True)
    scale = jnp.exp(top - peak) / whole_sum

    def gradient(g, _):
        gout[part(g), :] = (es[part(g), :] * scale - spread[part(g), :]).astype(gout.dtype)
        return 0

    lax.fori_loop(0, steps, gradient, 0)
    grad_copy = pltpu.make_async_copy(gout, grad_hbm, grad_sem)
    grad_copy.start()

    take(pick_buf, shards - 1, pick_sem)
    loss = peak + jnp.log(whole_sum) - jnp.sum(pick_buf[...], axis=0)
    loss_ref[...] = loss
    own_mean = jnp.broadcast_to(jnp.sum(loss, axis=1, keepdims=True), (1, LANES))
    mean_send[...] = own_mean
    mean_buf[pl.ds(my_dp, 1)] = own_mean.reshape(1, 1, LANES)
    cast(mean_send, mean_buf, 3, mean_sem, "dp", my_dp, groups)
    take(mean_buf, groups - 1, mean_sem)
    mean_ref[...] = jnp.sum(mean_buf[...], axis=0) / (groups * pos)

    take(outbuf, groups - 1, send_sem.at[0])
    take(stat_buf, shards - 1, send_sem.at[1])
    take(pick_buf, shards - 1, send_sem.at[2])
    take(mean_buf, groups - 1, send_sem.at[3])
    grad_copy.wait()


def solution(mesh):
    groups, shards = mesh.shape["dp"], mesh.shape["tensor"]

    def body(logits, child_ids, leaf_counts, leaf_valid, leaf_temp, leaf_owner):
        pos, cols = logits.shape
        child = child_ids.shape[1]
        cap = pos // groups
        padded = pl.cdiv(cols, WIDE) * WIDE
        vmem = pl.BlockSpec(memory_space=pltpu.VMEM)
        anywhere = pl.BlockSpec(memory_space=pl.ANY)
        gradient, row_loss, mean_loss = pl.pallas_call(
            functools.partial(kernel, groups, shards),
            out_shape=(
                jax.ShapeDtypeStruct((cols, pos), logits.dtype),
                jax.ShapeDtypeStruct((1, pos), F32),
                jax.ShapeDtypeStruct((1, LANES), F32),
            ),
            in_specs=[anywhere] + [vmem] * 5,
            out_specs=(anywhere, vmem, vmem),
            scratch_shapes=[
                pltpu.VMEM((cols, pos), logits.dtype),
                pltpu.VMEM((cols, pos), F32),
                pltpu.VMEM((pos, padded), F32),
                pltpu.VMEM((cols, pos), F32),
                pltpu.VMEM((cols, pos), logits.dtype),
                pltpu.VMEM((groups, cap, 2 * child), F32),
                pltpu.VMEM((groups, cap, 2 * child), F32),
                pltpu.VMEM((pos, 2 * LANES), F32),
                pltpu.VMEM((pos, LANES), jnp.int32),
                pltpu.VMEM((2, pos), F32),
                pltpu.VMEM((shards, 2, pos), F32),
                pltpu.VMEM((1, pos), F32),
                pltpu.VMEM((shards, 1, pos), F32),
                pltpu.VMEM((1, LANES), F32),
                pltpu.VMEM((groups, 1, LANES), F32),
                pltpu.SemaphoreType.DMA,
                pltpu.SemaphoreType.DMA,
                pltpu.SemaphoreType.DMA((4,)),
                pltpu.SemaphoreType.DMA,
                pltpu.SemaphoreType.DMA,
                pltpu.SemaphoreType.DMA,
                pltpu.SemaphoreType.DMA,
            ],
            compiler_params=pltpu.CompilerParams(collective_id=0, has_side_effects=True),
        )(
            logits.T, child_ids.T, leaf_counts.T,
            leaf_valid.reshape(1, pos), leaf_temp.reshape(1, pos), leaf_owner.reshape(1, pos),
        )
        return gradient.T, row_loss.reshape(pos), mean_loss[0, 0]

    return jax.shard_map(
        body,
        mesh=mesh,
        in_specs=(P("dp", "tensor"), P("dp", None), P("dp", None), P("dp"), P("dp"), P("dp")),
        out_specs=(P("dp", "tensor"), P("dp"), P()),
        check_vma=False,
    )
```

time: 134 us -> 57.3 us (0.43)
  other arithmetic: 65.6 us -> 0 us
  Pallas kernels: 0 us -> 51.4 us
  blocking collectives: 34 us -> 0 us
  starting transfers between devices: 14.8 us -> 0 us
  waiting for transfers between devices: 8.12 us -> 0 us
  local copies, waits for them, and re-layouts: 6.81 us -> 3.84 us
  matrix products: 1.43 us -> 0 us
    reduce_sum x6 -> x0, other arithmetic: 54.5 us -> none  [the longest x1 51.1 us: body(): jnp.sum(jnp.where(matches, targets[:, None, :], jnp.float32(0.0)), axis=2)]
    pallas_call x0 -> x1, Pallas kernels: none -> 51.4 us  [body(): pl.pallas_call(functools.partial(kernel, groups, shards), out_shape=(jax....]
    all_to_all x1 -> x0, blocking collectives: 34 us -> none  [sent_to_all(): lax.all_to_all(jnp.broadcast_to(value[None], (count, *value.shape)), axis...]
    all_to_all x3 -> x0, starting transfers between devices: 14.8 us -> none  [the longest x1 7.57 us: body(): lax.all_to_all(labels, 'dp', split_axis=0, concat_axis=0, tiled=True)]
    all_to_all x3 -> x0, waiting for transfers between devices: 8.12 us -> none  [the longest x1 4.53 us: body(): lax.all_to_all(labels, 'dp', split_axis=0, concat_axis=0, tiled=True)]
    convert_element_type x3 -> x0, other arithmetic: 4.85 us -> none  [the longest x1 4.84 us: body(): (jnp.exp(values - row_top[:, None]) * scale[:, None] - target_dense).asty...]
    reduce_max x1 -> x0, other arithmetic: 2.33 us -> none  [body(): own_top_narrow = jnp.max(logits, axis=1)]
    all_to_all x3 -> x0, local copies, waits for them, and re-layouts: 1.72 us -> none  [the longest x2 1.2 us: body(): lax.all_to_all(labels, 'dp', split_axis=0, concat_axis=0, tiled=True)]
  transfers between devices with their start and end apart: 3 -> 0, of which waited for: 3 -> 0; matrix products, arithmetic and copies ran while one was open for 8% -> 0% of each run, Pallas kernels for 0% -> 0%
where the time goes in v1:
time: 57.3 us; the launch traced here: 57 us
  Pallas kernels  51.4 us (90%)
  local copies, waits for them, and re-layouts  3.84 us (7%)
  between operations  1.82 us (3%)
    pallas_call x1, Pallas kernels, body(): pl.pallas_call(functools.partial(kernel, groups, shards), out_shape=(jax....  51.4 us
    unnamed x6, local copies, waits for them, and re-layouts  3.84 us

profile of v1, /device:TPU:1, one launch (start us, length us, event | category | flops | bytes accessed | tf_op | source)
XLA Modules:
  0.0 57.0 jit_solution(4097356995634915773)
XLA Ops:
  0.6 51.4 %shard_map.85 = (bf16[4752,256]{1,0:T(8,128)(2,1)}, f32[1,256]{1,0:T(1,128)}, f32[1,128]{1,0:T(1,128)}) custom-call(bf16[4752,256]{1,0:T(8,128)(2,1)} %bitcast.11, s32[64,256]{1,0:T(8,128)} %bitcast.12, s32[64,256]{1,0:T(8,128)} %bitcast.13, s32[1,256]{1,0:T(1,128)} %bitcast.14, f32[1,256]{1,0:T(1,128)} %bitcast.15, s32[1,256]{1,0:T(1,128)} %bitcast.16), custom_call_target="tpu_custom_call" | custom-call | tf_op jit(solution)/shard_map/pallas_call | solution.py:245
  52.0 0.0 copy-start
  52.0 0.0 copy-start.1
  52.0 3.3 %copy.12 = bf16[256,4752]{0,1:T(8,128)(2,1)} copy(bf16[256,4752]{0,1:T(8,128)(2,1)} %bitcast.10) | data formatting | bytes 4866048
  55.3 0.0 copy-done
  55.3 0.6 copy.13
  55.9 0.0 copy-done.1
Async XLA Ops:
  52.0 3.3 %copy-start = (f32[1,256]{1,0:T(1,128)S(1)}, f32[1,256]{1,0:T(1,128)}, u32[]{:S(2)}) copy-start(f32[1,256]{1,0:T(1,128)} %get-tuple-element.7) | copy-start | bytes 3076
  52.0 3.9 %copy-start.1 = (f32[1,128]{1,0:T(1,128)S(1)}, f32[1,128]{1,0:T(1,128)}, u32[]{:S(2)}) copy-start(f32[1,128]{1,0:T(1,128)} %get-tuple-element.8) | copy-start | bytes 1540

commit v2 on v1

--- a/solution.py
+++ b/solution.py
@@ -13,6 +13,7 @@
 LANES = 128
 WIDE = 256
 CHUNK = 176
+HEADS = 24
 
 
 def dot_nt(lhs, rhs):
@@ -33,10 +34,10 @@
 def kernel(
     groups, shards,
     x_hbm, ids_ref, count_ref, valid_ref, temp_ref, owner_ref,
-    grad_hbm, loss_ref, mean_ref,
-    xs, es, dense, spread, gout, outbuf, inbuf, placed, ids_rows,
+    gout, loss_ref, mean_ref,
+    xs, es, dense, turned_x, outbuf, inbuf, head_rows, rest_rows, at_ids, parts,
     stat_send, stat_buf, pick_send, pick_buf, mean_send, mean_buf,
-    x_sem, grad_sem, send_sem, route_sem, stat_sem, pick_sem, mean_sem,
+    x_sem, send_sem, route_sem, stat_sem, pick_sem, mean_sem,
 ):
     cols, pos = x_hbm.shape
     child = ids_ref.shape[0]
@@ -45,7 +46,7 @@
     my_t = lax.axis_index("tensor")
     heads = pl.cdiv(cols, WIDE)
 
-    x_copy = pltpu.make_async_copy(x_hbm, xs, x_sem)
+    x_copy = pltpu.make_async_copy(x_hbm, xs.at[pl.ds(0, cols)], x_sem)
     x_copy.start()
 
     barrier = pltpu.get_barrier_semaphore()
@@ -82,8 +83,13 @@
     outgoing = outgoing + dot_nt(sender, jnp.concatenate([low, none], axis=0))
     outbuf[...] = outgoing.reshape(groups, cap, 2 * child)
 
+    pairs = pos // 2
     local = ids_ref[...] - my_t * cols
-    ids_rows[...] = jnp.transpose(jnp.concatenate([local, local], axis=0))
+    local = jnp.concatenate([local[:, :pairs], local[:, pairs:]], axis=0)
+    local = jnp.transpose(local)
+    head = lax.shift_right_arithmetic(local, 8)
+    head_rows[...] = jnp.where((head >= 0) & (head < heads), head, -1).astype(F32)
+    rest_rows[...] = lax.bitwise_and(local, WIDE - 1).astype(F32)
 
     x_copy.wait()
     steps = cols // CHUNK
@@ -138,68 +144,92 @@
     cast(stat_send, stat_buf, 1, stat_sem, "tensor", my_t, shards)
     inbuf[pl.ds(my_dp, 1)] = outbuf[pl.ds(my_dp, 1)]
 
+    xs[cols:, :] = jnp.zeros((xs.shape[0] - cols, pos), xs.dtype)
+
+    def turn(h, _):
+        tile = xs[pl.ds(pl.multiple_of(h * WIDE, WIDE), WIDE), :].astype(F32)
+        tile = jnp.transpose(tile)
+        for c in range(WIDE // LANES):
+            turned_x[c, pl.ds(h, pos, stride=HEADS), :] = tile[:, c * LANES : (c + 1) * LANES]
+        return 0
+
+    lax.fori_loop(0, heads, turn, 0)
+
+    spread_rows = iota((WIDE, LANES), 0).astype(F32).astype(BF16)
+    one = jnp.ones((WIDE, LANES), BF16)
+    nil = jnp.zeros((WIDE, LANES), BF16)
+    head_index = iota((2 * HEADS, LANES), 0)
+    lane = iota((2 * HEADS, LANES), 1)
+    second = lane >= child
+    head_index = jnp.where(
+        second, jnp.where(head_index >= HEADS, head_index - HEADS, -2), jnp.where(head_index < HEADS, head_index, -2)
+    ).astype(F32)
+    batch = 8
+
+    def pair_onehot(rest, k):
+        row = rest[k : k + 1].astype(BF16)
+        return jnp.where(spread_rows == row, one, nil)
+
+    def pair_rows(at):
+        first = pl.multiple_of(at * HEADS, 8)
+        return pl.ds(first, HEADS), pl.ds(pl.multiple_of(first + pairs * HEADS, 8), HEADS)
+
+    def joined(ref, rows):
+        return jnp.concatenate([ref[c, rows, :] for c in range(WIDE // LANES)], axis=1)
+
+    def gather(g, _):
+        rows = pl.ds(pl.multiple_of(g * batch, batch), batch)
+        head, rest = head_rows[rows, :], rest_rows[rows, :]
+        found = []
+        for k in range(batch):
+            upper, lower = pair_rows(g * batch + k)
+            values = jnp.concatenate([joined(turned_x, upper), joined(turned_x, lower)], axis=0).astype(BF16)
+            reached = jnp.dot(values, pair_onehot(rest, k), preferred_element_type=F32)
+            hit = head_index == head[k : k + 1]
+            found.append(jnp.sum(jnp.where(hit, reached, 0.0), axis=0, keepdims=True))
+        at_ids[rows, :] = jnp.concatenate(found, axis=0)
+        return 0
+
+    lax.fori_loop(0, pairs // batch, gather, 0)
+
     take(inbuf, groups - 1, route_sem)
     turned = jnp.transpose(inbuf[...].reshape(pos, 2 * child))
-    high, middle, low = split(turned[:child])
     label = turned[child : child + 1].astype(jnp.int32)
     receiver = jnp.where(iota((pos, pos), 0) == label, 1.0, 0.0).astype(BF16)
-    placed[...] = dot_nt(receiver, jnp.concatenate([high, middle, low, low], axis=0))
-
-    block = 8
-    width = block * child
-    lane = iota((block, LANES), 1)
-    half = (lane >= child).astype(jnp.int32)
-    row8 = iota((block, LANES), 0)
-    per = LANES // child
-    pieces = width // LANES
-    spread_rows = iota((WIDE, width), 0)
-
-    def target_rows(g, _):
-        rows = pl.ds(pl.multiple_of(g * block, block), block)
-        local = ids_rows[rows, :]
-        head = lax.shift_right_arithmetic(local, 8)
-        rest = lax.bitwise_and(local, WIDE - 1)
-        parts = placed[rows, 0:LANES]
-        swapped = pltpu.roll(parts, child, 1)
-        high2 = jnp.where(lane < child, parts, swapped)
-        middle2 = jnp.where(lane < child, swapped, parts)
-        low2 = placed[rows, LANES : 2 * LANES]
-        heads_at, rests_at = [], []
-        for c in range(pieces):
-            own = row8 == per * c + half
-            heads_at.append(jnp.where(own, head, -1))
-            rests_at.append(jnp.sum(jnp.where(own, rest, 0), axis=0, keepdims=True))
-        onehot = jnp.where(spread_rows == jnp.concatenate(rests_at, axis=1), 1.0, 0.0).astype(BF16)
-        hits = [[at == h for at in heads_at] for h in range(heads)]
-        found = jnp.zeros((heads * block, WIDE), F32)
-        for value in (high2, middle2, low2):
-            chosen = [jnp.concatenate([jnp.where(at, value, 0.0) for at in hit], axis=1) for hit in hits]
-            found = found + dot_nt(jnp.concatenate(chosen, axis=0).astype(BF16), onehot)
-        for h in range(heads):
-            dense[rows, h * WIDE : (h + 1) * WIDE] = found[h * block : (h + 1) * block]
-        return 0
-
-    lax.fori_loop(0, pos // block, target_rows, 0)
-
-    def turn(b, total):
-        at = pl.multiple_of(b * LANES, LANES)
-        tile = jnp.transpose(dense[:, pl.ds(at, LANES)])
-        spread[pl.ds(at, LANES), :] = tile
-        product = tile * xs[pl.ds(at, LANES), :].astype(F32)
-        return total + jnp.sum(product.reshape(LANES // 8, 8, pos), axis=0)
-
-    whole = cols // LANES
-    total = lax.fori_loop(0, whole, turn, jnp.zeros((8, pos), F32))
-    left = cols - whole * LANES
-    if left:
-        tile = jnp.transpose(dense[:, whole * LANES : (whole + 1) * LANES])[:left]
-        spread[whole * LANES : cols, :] = tile
-        product = tile * xs[whole * LANES : cols, :].astype(F32)
-        total = total + jnp.sum(product.reshape(left // 8, 8, pos), axis=0)
-    own_pick = jnp.sum(total, axis=0, keepdims=True)
+    wanted = [part for part in split(turned[:child]) for _ in range(LANES // child)]
+    placed = dot_nt(receiver, jnp.concatenate(wanted, axis=0))
+    first_half = iota((pairs, LANES), 1) < child
+    target = jnp.zeros((pairs, LANES), F32)
+    for k in range(3):
+        both = placed[:, k * LANES : (k + 1) * LANES]
+        both = jnp.where(first_half, both[:pairs], both[pairs:])
+        parts[k] = both
+        target = target + both
+    product = jnp.transpose(target * at_ids[...])
+    own_pick = jnp.concatenate(
+        [jnp.sum(product[:child], axis=0, keepdims=True), jnp.sum(product[child:], axis=0, keepdims=True)], axis=1
+    )
     pick_send[...] = own_pick
     pick_buf[pl.ds(my_t, 1)] = own_pick.reshape(1, 1, pos)
     cast(pick_send, pick_buf, 2, pick_sem, "tensor", my_t, shards)
+
+    def spread(g, _):
+        rows = pl.ds(pl.multiple_of(g * batch, batch), batch)
+        head, rest = head_rows[rows, :], rest_rows[rows, :]
+        values = [parts[k, rows, :] for k in range(3)]
+        for k in range(batch):
+            hit = head_index == head[k : k + 1]
+            chosen = jnp.concatenate([jnp.where(hit, value[k : k + 1], 0.0) for value in values], axis=0)
+            found = dot_nt(chosen.astype(BF16), pair_onehot(rest, k))
+            size = 2 * HEADS
+            found = found[:size] + found[size : 2 * size] + found[2 * size :]
+            upper, lower = pair_rows(g * batch + k)
+            for c in range(WIDE // LANES):
+                dense[c, upper, :] = found[:HEADS, c * LANES : (c + 1) * LANES]
+                dense[c, lower, :] = found[HEADS:, c * LANES : (c + 1) * LANES]
+        return 0
+
+    lax.fori_loop(0, pairs // batch, spread, 0)
 
     take(stat_buf, shards - 1, stat_sem)
     every_top, every_sum = stat_buf[:, 0, :], stat_buf[:, 1, :]
@@ -207,13 +237,18 @@
     whole_sum = jnp.sum(every_sum * jnp.exp(every_top - peak), axis=0, keepdims=True)
     scale = jnp.exp(top - peak) / whole_sum
 
-    def gradient(g, _):
-        gout[part(g), :] = (es[part(g), :] * scale - spread[part(g), :]).astype(gout.dtype)
-        return 0
-
-    lax.fori_loop(0, steps, gradient, 0)
-    grad_copy = pltpu.make_async_copy(gout, grad_hbm, grad_sem)
-    grad_copy.start()
+    def gradient(h, rows, size):
+        tile = jnp.transpose(joined(dense, pl.ds(h, pos, stride=HEADS)))[:size]
+        gout[rows, :] = (es[rows, :] * scale - tile).astype(gout.dtype)
+
+    def gradient_step(h, _):
+        gradient(h, pl.ds(pl.multiple_of(h * WIDE, WIDE), WIDE), WIDE)
+        return 0
+
+    whole = cols // WIDE
+    lax.fori_loop(0, whole, gradient_step, 0)
+    if cols > whole * WIDE:
+        gradient(whole, pl.ds(whole * WIDE, cols - whole * WIDE), cols - whole * WIDE)
 
     take(pick_buf, shards - 1, pick_sem)
     loss = peak + jnp.log(whole_sum) - jnp.sum(pick_buf[...], axis=0)
@@ -229,7 +264,6 @@
     take(stat_buf, shards - 1, send_sem.at[1])
     take(pick_buf, shards - 1, send_sem.at[2])
     take(mean_buf, groups - 1, send_sem.at[3])
-    grad_copy.wait()
 
 
 def solution(mesh):
@@ -245,29 +279,29 @@
         gradient, row_loss, mean_loss = pl.pallas_call(
             functools.partial(kernel, groups, shards),
             out_shape=(
-                jax.ShapeDtypeStruct((cols, pos), logits.dtype),
-                jax.ShapeDtypeStruct((1, pos), F32),
-                jax.ShapeDtypeStruct((1, LANES), F32),
+                pltpu.VMEM((cols, pos), logits.dtype),
+                pltpu.VMEM((1, pos), F32),
+                pltpu.VMEM((1, LANES), F32),
             ),
             in_specs=[anywhere] + [vmem] * 5,
-            out_specs=(anywhere, vmem, vmem),
+            out_specs=(vmem, vmem, vmem),
             scratch_shapes=[
-                pltpu.VMEM((cols, pos), logits.dtype),
+                pltpu.VMEM((padded, pos), logits.dtype),
                 pltpu.VMEM((cols, pos), F32),
-                pltpu.VMEM((pos, padded), F32),
-                pltpu.VMEM((cols, pos), F32),
-                pltpu.VMEM((cols, pos), logits.dtype),
+                pltpu.VMEM((WIDE // LANES, pos * HEADS, LANES), F32),
+                pltpu.VMEM((WIDE // LANES, pos * HEADS, LANES), F32),
                 pltpu.VMEM((groups, cap, 2 * child), F32),
                 pltpu.VMEM((groups, cap, 2 * child), F32),
-                pltpu.VMEM((pos, 2 * LANES), F32),
-                pltpu.VMEM((pos, LANES), jnp.int32),
+                pltpu.VMEM((pos // 2, LANES), F32),
+                pltpu.VMEM((pos // 2, LANES), F32),
+                pltpu.VMEM((pos // 2, LANES), F32),
+                pltpu.VMEM((3, pos // 2, LANES), F32),
                 pltpu.VMEM((2, pos), F32),
                 pltpu.VMEM((shards, 2, pos), F32),
                 pltpu.VMEM((1, pos), F32),
                 pltpu.VMEM((shards, 1, pos), F32),
                 pltpu.VMEM((1, LANES), F32),
                 pltpu.VMEM((groups, 1, LANES), F32),
-                pltpu.SemaphoreType.DMA,
                 pltpu.SemaphoreType.DMA,
                 pltpu.SemaphoreType.DMA((4,)),
                 pltpu.SemaphoreType.DMA,

time: 57.3 us -> 42.6 us (0.74)
  Pallas kernels: 51.4 us -> 38.6 us
  local copies, waits for them, and re-layouts: 3.84 us -> 1.99 us
    pallas_call x1, Pallas kernels: 51.4 us -> 38.6 us  [body(): pl.pallas_call(functools.partial(kernel, groups, shards), out_shape=(pltp...]
    unnamed x6 -> x2, local copies, waits for them, and re-layouts: 3.84 us -> 1.99 us
where the time goes in v2:
time: 42.6 us; the launch traced here: 42.4 us
  Pallas kernels  38.6 us (91%)
  local copies, waits for them, and re-layouts  1.99 us (5%)
  between operations  1.81 us (4%)
    pallas_call x1, Pallas kernels, body(): pl.pallas_call(functools.partial(kernel, groups, shards), out_shape=(pltp...  38.6 us
    unnamed x2, local copies, waits for them, and re-layouts  1.99 us

profile of v2, /device:TPU:1, one launch (start us, length us, event | category | flops | bytes accessed | tf_op | source)
XLA Modules:
  0.0 42.4 jit_solution(11449074317642884508)
XLA Ops:
  0.6 38.6 %shard_map.85 = (bf16[4752,256]{1,0:T(8,128)(2,1)S(1)}, f32[1,256]{1,0:T(1,128)S(1)}, f32[1,128]{1,0:T(1,128)S(1)}) custom-call(bf16[4752,256]{1,0:T(8,128)(2,1)} %bitcast.13, s32[64,256]{1,0:T(8,128)} %bitcast.14, s32[64,256]{1,0:T(8,128)} %bitcast.15, s32[1,256]{1,0:T(1,128)} %bitcast.16, f32[1,256]{1,0:T(1,128)} %bitcast.17, s32[1,256]{1,0:T(1,128)} %bitcast.18), custom_call_target="tpu_custom_call" | custom-call | tf_op jit(solution)/shard_map/pallas_call | solution.py:279
  39.3 1.4 %copy.12 = bf16[256,4752]{0,1:T(8,128)(2,1)} copy(bf16[256,4752]{0,1:T(8,128)(2,1)S(1)} %bitcast.10) | data formatting | bytes 4866048
  40.7 0.6 %copy.13 = f32[256]{0:T(256)} copy(f32[256]{0:T(256)S(1)} %bitcast.11) | data formatting | bytes 2048

commit v3 on v2

--- a/solution.py
+++ b/solution.py
@@ -27,6 +27,22 @@
     return high, middle, (rest - middle.astype(F32)).astype(BF16)
 
 
+def from_afar(step, count):
+    away = lax.div(step + 1, 2)
+    return count // 2 + jnp.where(lax.rem(step, 2) == 0, -away, away)
+
+
+def repeat(count, factor, step):
+    def trip(g, _):
+        for k in range(factor):
+            step(g * factor + k)
+        return 0
+
+    lax.fori_loop(0, count // factor, trip, 0)
+    for k in range(count // factor * factor, count):
+        step(k)
+
+
 def iota(shape, dim):
     return lax.broadcasted_iota(jnp.int32, shape, dim)
 
@@ -36,8 +52,8 @@
     x_hbm, ids_ref, count_ref, valid_ref, temp_ref, owner_ref,
     gout, loss_ref, mean_ref,
     xs, es, dense, turned_x, outbuf, inbuf, head_rows, rest_rows, at_ids, parts,
-    stat_send, stat_buf, pick_send, pick_buf, mean_send, mean_buf,
-    x_sem, send_sem, route_sem, stat_sem, pick_sem, mean_sem,
+    stat_send, stat_buf, mean_send, mean_buf,
+    x_sem, send_sem, route_sem, stat_sem, mean_sem,
 ):
     cols, pos = x_hbm.shape
     child = ids_ref.shape[0]
@@ -51,16 +67,19 @@
 
     barrier = pltpu.get_barrier_semaphore()
 
+    def peer_of(me, k, count):
+        return lax.rem(me + from_afar(k, count), count)
+
+    def greet_t(k, _):
+        pl.semaphore_signal(barrier, inc=1, device_id={"tensor": peer_of(my_t, k, shards)}, device_id_type=MESH)
+        return 0
+
     def greet_dp(k, _):
-        pl.semaphore_signal(barrier, inc=1, device_id={"dp": lax.rem(my_dp + k, groups)}, device_id_type=MESH)
+        pl.semaphore_signal(barrier, inc=1, device_id={"dp": peer_of(my_dp, k, groups)}, device_id_type=MESH)
         return 0
 
-    def greet_t(k, _):
-        pl.semaphore_signal(barrier, inc=1, device_id={"tensor": lax.rem(my_t + k, shards)}, device_id_type=MESH)
-        return 0
-
-    lax.fori_loop(1, groups, greet_dp, 0)
-    lax.fori_loop(1, shards, greet_t, 0)
+    lax.fori_loop(0, shards - 1, greet_t, 0)
+    lax.fori_loop(0, groups - 1, greet_dp, 0)
 
     powered = jnp.exp(jnp.log(count_ref[...].astype(F32)) * temp_ref[...])
     weights = jnp.where(iota((child, pos), 0) < valid_ref[...], powered, 0.0)
@@ -112,14 +131,22 @@
         return total + jnp.sum(fold(powers), axis=0)
 
     total = lax.fori_loop(0, steps, sums, jnp.zeros((8, pos), F32))
-    own_stats = jnp.concatenate([top, jnp.sum(total, axis=0, keepdims=True)], axis=0)
-    stat_send[...] = own_stats
-    stat_buf[pl.ds(my_t, 1)] = own_stats.reshape(1, 2, pos)
+    own_sum = jnp.sum(total, axis=0, keepdims=True)
+
+    xs[cols:, :] = jnp.zeros((xs.shape[0] - cols, pos), xs.dtype)
+
+    def turn(h):
+        at = h * WIDE if isinstance(h, int) else pl.multiple_of(h * WIDE, WIDE)
+        tile = jnp.transpose(xs[pl.ds(at, WIDE), :]).astype(F32)
+        for c in range(WIDE // LANES):
+            turned_x[c, pl.ds(h, pos, stride=HEADS), :] = tile[:, c * LANES : (c + 1) * LANES]
+
+    repeat(heads, 3, turn)
 
     pl.semaphore_wait(barrier, groups - 1 + shards - 1)
 
     def route(k, _):
-        peer = lax.rem(my_dp + k, groups)
+        peer = peer_of(my_dp, k, groups)
         pltpu.make_async_remote_copy(
             outbuf.at[peer], inbuf.at[my_dp], send_sem.at[0], route_sem,
             device_id={"dp": peer}, device_id_type=MESH,
@@ -130,30 +157,18 @@
         def one(k, _):
             pltpu.make_async_remote_copy(
                 source, buffer.at[me], send_sem.at[slot], sem,
-                device_id={axis: lax.rem(me + k, count)}, device_id_type=MESH,
+                device_id={axis: peer_of(me, k, count)}, device_id_type=MESH,
             ).start()
             return 0
 
-        lax.fori_loop(1, count, one, 0)
+        lax.fori_loop(0, count - 1, one, 0)
 
     def take(buffer, count, sem):
         piece = buffer.at[pl.ds(0, count)]
         pltpu.make_async_copy(piece, piece, sem).wait()
 
-    lax.fori_loop(1, groups, route, 0)
-    cast(stat_send, stat_buf, 1, stat_sem, "tensor", my_t, shards)
+    lax.fori_loop(0, groups - 1, route, 0)
     inbuf[pl.ds(my_dp, 1)] = outbuf[pl.ds(my_dp, 1)]
-
-    xs[cols:, :] = jnp.zeros((xs.shape[0] - cols, pos), xs.dtype)
-
-    def turn(h, _):
-        tile = xs[pl.ds(pl.multiple_of(h * WIDE, WIDE), WIDE), :].astype(F32)
-        tile = jnp.transpose(tile)
-        for c in range(WIDE // LANES):
-            turned_x[c, pl.ds(h, pos, stride=HEADS), :] = tile[:, c * LANES : (c + 1) * LANES]
-        return 0
-
-    lax.fori_loop(0, heads, turn, 0)
 
     spread_rows = iota((WIDE, LANES), 0).astype(F32).astype(BF16)
     one = jnp.ones((WIDE, LANES), BF16)
@@ -177,7 +192,7 @@
     def joined(ref, rows):
         return jnp.concatenate([ref[c, rows, :] for c in range(WIDE // LANES)], axis=1)
 
-    def gather(g, _):
+    def gather(g):
         rows = pl.ds(pl.multiple_of(g * batch, batch), batch)
         head, rest = head_rows[rows, :], rest_rows[rows, :]
         found = []
@@ -188,9 +203,8 @@
             hit = head_index == head[k : k + 1]
             found.append(jnp.sum(jnp.where(hit, reached, 0.0), axis=0, keepdims=True))
         at_ids[rows, :] = jnp.concatenate(found, axis=0)
-        return 0
-
-    lax.fori_loop(0, pairs // batch, gather, 0)
+
+    repeat(pairs // batch, 8, gather)
 
     take(inbuf, groups - 1, route_sem)
     turned = jnp.transpose(inbuf[...].reshape(pos, 2 * child))
@@ -209,11 +223,12 @@
     own_pick = jnp.concatenate(
         [jnp.sum(product[:child], axis=0, keepdims=True), jnp.sum(product[child:], axis=0, keepdims=True)], axis=1
     )
-    pick_send[...] = own_pick
-    pick_buf[pl.ds(my_t, 1)] = own_pick.reshape(1, 1, pos)
-    cast(pick_send, pick_buf, 2, pick_sem, "tensor", my_t, shards)
-
-    def spread(g, _):
+    own_stats = jnp.concatenate([top, own_sum, own_pick], axis=0)
+    stat_send[...] = own_stats
+    stat_buf[pl.ds(my_t, 1)] = own_stats.reshape(1, 3, pos)
+    cast(stat_send, stat_buf, 1, stat_sem, "tensor", my_t, shards)
+
+    def spread(g):
         rows = pl.ds(pl.multiple_of(g * batch, batch), batch)
         head, rest = head_rows[rows, :], rest_rows[rows, :]
         values = [parts[k, rows, :] for k in range(3)]
@@ -227,43 +242,39 @@
             for c in range(WIDE // LANES):
                 dense[c, upper, :] = found[:HEADS, c * LANES : (c + 1) * LANES]
                 dense[c, lower, :] = found[HEADS:, c * LANES : (c + 1) * LANES]
-        return 0
-
-    lax.fori_loop(0, pairs // batch, spread, 0)
+
+    repeat(pairs // batch, 4, spread)
 
     take(stat_buf, shards - 1, stat_sem)
     every_top, every_sum = stat_buf[:, 0, :], stat_buf[:, 1, :]
     peak = jnp.max(every_top, axis=0, keepdims=True)
     whole_sum = jnp.sum(every_sum * jnp.exp(every_top - peak), axis=0, keepdims=True)
-    scale = jnp.exp(top - peak) / whole_sum
-
-    def gradient(h, rows, size):
-        tile = jnp.transpose(joined(dense, pl.ds(h, pos, stride=HEADS)))[:size]
-        gout[rows, :] = (es[rows, :] * scale - tile).astype(gout.dtype)
-
-    def gradient_step(h, _):
-        gradient(h, pl.ds(pl.multiple_of(h * WIDE, WIDE), WIDE), WIDE)
-        return 0
-
-    whole = cols // WIDE
-    lax.fori_loop(0, whole, gradient_step, 0)
-    if cols > whole * WIDE:
-        gradient(whole, pl.ds(whole * WIDE, cols - whole * WIDE), cols - whole * WIDE)
-
-    take(pick_buf, shards - 1, pick_sem)
-    loss = peak + jnp.log(whole_sum) - jnp.sum(pick_buf[...], axis=0)
+    loss = peak + jnp.log(whole_sum) - jnp.sum(stat_buf[:, 2, :], axis=0, keepdims=True)
     loss_ref[...] = loss
     own_mean = jnp.broadcast_to(jnp.sum(loss, axis=1, keepdims=True), (1, LANES))
     mean_send[...] = own_mean
     mean_buf[pl.ds(my_dp, 1)] = own_mean.reshape(1, 1, LANES)
-    cast(mean_send, mean_buf, 3, mean_sem, "dp", my_dp, groups)
+    cast(mean_send, mean_buf, 2, mean_sem, "dp", my_dp, groups)
+
+    scale = jnp.exp(top - peak) / whole_sum
+
+    def gradient(h, size=WIDE):
+        at = h * WIDE if isinstance(h, int) else pl.multiple_of(h * WIDE, WIDE)
+        rows = pl.ds(at, size)
+        tile = jnp.transpose(joined(dense, pl.ds(h, pos, stride=HEADS)))[:size]
+        gout[rows, :] = (es[rows, :] * scale - tile).astype(gout.dtype)
+
+    whole = cols // WIDE
+    repeat(whole, 6, gradient)
+    if cols > whole * WIDE:
+        gradient(whole, cols - whole * WIDE)
+
     take(mean_buf, groups - 1, mean_sem)
     mean_ref[...] = jnp.sum(mean_buf[...], axis=0) / (groups * pos)
 
     take(outbuf, groups - 1, send_sem.at[0])
     take(stat_buf, shards - 1, send_sem.at[1])
-    take(pick_buf, shards - 1, send_sem.at[2])
-    take(mean_buf, groups - 1, send_sem.at[3])
+    take(mean_buf, groups - 1, send_sem.at[2])
 
 
 def solution(mesh):
@@ -296,15 +307,12 @@
                 pltpu.VMEM((pos // 2, LANES), F32),
                 pltpu.VMEM((pos // 2, LANES), F32),
                 pltpu.VMEM((3, pos // 2, LANES), F32),
-                pltpu.VMEM((2, pos), F32),
-                pltpu.VMEM((shards, 2, pos), F32),
-                pltpu.VMEM((1, pos), F32),
-                pltpu.VMEM((shards, 1, pos), F32),
+                pltpu.VMEM((3, pos), F32),
+                pltpu.VMEM((shards, 3, pos), F32),
                 pltpu.VMEM((1, LANES), F32),
                 pltpu.VMEM((groups, 1, LANES), F32),
                 pltpu.SemaphoreType.DMA,
-                pltpu.SemaphoreType.DMA((4,)),
-                pltpu.SemaphoreType.DMA,
+                pltpu.SemaphoreType.DMA((3,)),
                 pltpu.SemaphoreType.DMA,
                 pltpu.SemaphoreType.DMA,
                 pltpu.SemaphoreType.DMA,

time: 42.6 us -> 38.5 us (0.904)
  Pallas kernels: 38.6 us -> 34.5 us
    pallas_call x1, Pallas kernels: 38.6 us -> 34.5 us  [body(): pl.pallas_call(functools.partial(kernel, groups, shards), out_shape=(pltp...]
where the time goes in v3:
time: 38.5 us; the launch traced here: 38.3 us
  Pallas kernels  34.5 us (90%)
  local copies, waits for them, and re-layouts  1.99 us (5%)
  between operations  1.81 us (5%)
    pallas_call x1, Pallas kernels, body(): pl.pallas_call(functools.partial(kernel, groups, shards), out_shape=(pltp...  34.5 us
    unnamed x2, local copies, waits for them, and re-layouts  1.99 us

profile of v3, /device:TPU:1, one launch (start us, length us, event | category | flops | bytes accessed | tf_op | source)
XLA Modules:
  0.0 38.3 jit_solution(5885320725137236373)
XLA Ops:
  0.6 34.5 %shard_map.85 = (bf16[4752,256]{1,0:T(8,128)(2,1)S(1)}, f32[1,256]{1,0:T(1,128)S(1)}, f32[1,128]{1,0:T(1,128)S(1)}) custom-call(bf16[4752,256]{1,0:T(8,128)(2,1)} %bitcast.13, s32[64,256]{1,0:T(8,128)} %bitcast.14, s32[64,256]{1,0:T(8,128)} %bitcast.15, s32[1,256]{1,0:T(1,128)} %bitcast.16, f32[1,256]{1,0:T(1,128)} %bitcast.17, s32[1,256]{1,0:T(1,128)} %bitcast.18), custom_call_target="tpu_custom_call" | custom-call | tf_op jit(solution)/shard_map/pallas_call | solution.py:290
  35.2 1.4 %copy.12 = bf16[256,4752]{0,1:T(8,128)(2,1)} copy(bf16[256,4752]{0,1:T(8,128)(2,1)S(1)} %bitcast.10) | data formatting | bytes 4866048
  36.6 0.6 %copy.13 = f32[256]{0:T(256)} copy(f32[256]{0:T(256)S(1)} %bitcast.11) | data formatting | bytes 2048

commit v4 on v3

--- a/solution.py
+++ b/solution.py
@@ -27,9 +27,12 @@
     return high, middle, (rest - middle.astype(F32)).astype(BF16)
 
 
-def from_afar(step, count):
-    away = lax.div(step + 1, 2)
-    return count // 2 + jnp.where(lax.rem(step, 2) == 0, -away, away)
+def offsets(count):
+    return sorted(range(1, count), key=lambda k: -min(k, count - k))
+
+
+def near_offsets(count):
+    return [k for k in offsets(count) if min(k, count - k) <= count // 4 + 1]
 
 
 def repeat(count, factor, step):
@@ -53,7 +56,7 @@
     gout, loss_ref, mean_ref,
     xs, es, dense, turned_x, outbuf, inbuf, head_rows, rest_rows, at_ids, parts,
     stat_send, stat_buf, mean_send, mean_buf,
-    x_sem, send_sem, route_sem, stat_sem, mean_sem,
+    x_sem, send_sem, route_sem, stat_sem, mean_sem, hello_sem,
 ):
     cols, pos = x_hbm.shape
     child = ids_ref.shape[0]
@@ -68,18 +71,13 @@
     barrier = pltpu.get_barrier_semaphore()
 
     def peer_of(me, k, count):
-        return lax.rem(me + from_afar(k, count), count)
-
-    def greet_t(k, _):
+        return lax.rem(me + k, count)
+
+    near = near_offsets(shards)
+    for k in near:
         pl.semaphore_signal(barrier, inc=1, device_id={"tensor": peer_of(my_t, k, shards)}, device_id_type=MESH)
-        return 0
-
-    def greet_dp(k, _):
+    for k in offsets(groups):
         pl.semaphore_signal(barrier, inc=1, device_id={"dp": peer_of(my_dp, k, groups)}, device_id_type=MESH)
-        return 0
-
-    lax.fori_loop(0, shards - 1, greet_t, 0)
-    lax.fori_loop(0, groups - 1, greet_dp, 0)
 
     powered = jnp.exp(jnp.log(count_ref[...].astype(F32)) * temp_ref[...])
     weights = jnp.where(iota((child, pos), 0) < valid_ref[...], powered, 0.0)
@@ -119,11 +117,14 @@
     def fold(value):
         return value.reshape(CHUNK // 8, 8, pos)
 
+    def peaks(values):
+        return jnp.max(values.reshape(CHUNK // 16, 16, pos), axis=0)
+
     def tops(g, top):
-        return jnp.maximum(top, jnp.max(fold(xs[part(g), :].astype(F32)), axis=0))
-
-    top = lax.fori_loop(1, steps, tops, jnp.max(fold(xs[0:CHUNK, :].astype(F32)), axis=0))
-    top = jnp.max(top, axis=0, keepdims=True)
+        return jnp.maximum(top, peaks(xs[part(g), :]))
+
+    top = lax.fori_loop(1, steps, tops, peaks(xs[0:CHUNK, :]))
+    top = jnp.max(top.astype(F32), axis=0, keepdims=True)
 
     def sums(g, total):
         powers = jnp.exp(xs[part(g), :].astype(F32) - top)
@@ -132,6 +133,29 @@
 
     total = lax.fori_loop(0, steps, sums, jnp.zeros((8, pos), F32))
     own_sum = jnp.sum(total, axis=0, keepdims=True)
+
+    pl.semaphore_wait(barrier, groups - 1 + len(near))
+
+    def cast(source, buffer, slot, sem, axis, me, count):
+        for k in offsets(count):
+            pltpu.make_async_remote_copy(
+                source, buffer.at[me], send_sem.at[slot], sem,
+                device_id={axis: peer_of(me, k, count)}, device_id_type=MESH,
+            ).start()
+
+    def take(buffer, count, sem):
+        piece = buffer.at[pl.ds(0, count)]
+        pltpu.make_async_copy(piece, piece, sem).wait()
+
+    for k in offsets(groups):
+        peer = peer_of(my_dp, k, groups)
+        pltpu.make_async_remote_copy(
+            outbuf.at[peer], inbuf.at[my_dp], send_sem.at[0], route_sem,
+            device_id={"dp": peer}, device_id_type=MESH,
+        ).start()
+    for k in near:
+        pl.semaphore_signal(hello_sem, inc=1, device_id={"tensor": peer_of(my_t, k, shards)}, device_id_type=MESH)
+    inbuf[pl.ds(my_dp, 1)] = outbuf[pl.ds(my_dp, 1)]
 
     xs[cols:, :] = jnp.zeros((xs.shape[0] - cols, pos), xs.dtype)
 
@@ -142,33 +166,6 @@
             turned_x[c, pl.ds(h, pos, stride=HEADS), :] = tile[:, c * LANES : (c + 1) * LANES]
 
     repeat(heads, 3, turn)
-
-    pl.semaphore_wait(barrier, groups - 1 + shards - 1)
-
-    def route(k, _):
-        peer = peer_of(my_dp, k, groups)
-        pltpu.make_async_remote_copy(
-            outbuf.at[peer], inbuf.at[my_dp], send_sem.at[0], route_sem,
-            device_id={"dp": peer}, device_id_type=MESH,
-        ).start()
-        return 0
-
-    def cast(source, buffer, slot, sem, axis, me, count):
-        def one(k, _):
-            pltpu.make_async_remote_copy(
-                source, buffer.at[me], send_sem.at[slot], sem,
-                device_id={axis: peer_of(me, k, count)}, device_id_type=MESH,
-            ).start()
-            return 0
-
-        lax.fori_loop(0, count - 1, one, 0)
-
-    def take(buffer, count, sem):
-        piece = buffer.at[pl.ds(0, count)]
-        pltpu.make_async_copy(piece, piece, sem).wait()
-
-    lax.fori_loop(0, groups - 1, route, 0)
-    inbuf[pl.ds(my_dp, 1)] = outbuf[pl.ds(my_dp, 1)]
 
     spread_rows = iota((WIDE, LANES), 0).astype(F32).astype(BF16)
     one = jnp.ones((WIDE, LANES), BF16)
@@ -226,6 +223,7 @@
     own_stats = jnp.concatenate([top, own_sum, own_pick], axis=0)
     stat_send[...] = own_stats
     stat_buf[pl.ds(my_t, 1)] = own_stats.reshape(1, 3, pos)
+    pl.semaphore_wait(hello_sem, len(near))
     cast(stat_send, stat_buf, 1, stat_sem, "tensor", my_t, shards)
 
     def spread(g):
@@ -277,6 +275,16 @@
     take(mean_buf, groups - 1, send_sem.at[2])
 
 
+def leave(*refs):
+    count = len(refs) // 2
+    sems = refs[-1]
+    copies = [pltpu.make_async_copy(refs[k], refs[count + k], sems.at[k]) for k in range(count)]
+    for copy in copies:
+        copy.start()
+    for copy in copies:
+        copy.wait()
+
+
 def solution(mesh):
     groups, shards = mesh.shape["dp"], mesh.shape["tensor"]
 
@@ -287,7 +295,7 @@
         padded = pl.cdiv(cols, WIDE) * WIDE
         vmem = pl.BlockSpec(memory_space=pltpu.VMEM)
         anywhere = pl.BlockSpec(memory_space=pl.ANY)
-        gradient, row_loss, mean_loss = pl.pallas_call(
+        results = pl.pallas_call(
             functools.partial(kernel, groups, shards),
             out_shape=(
                 pltpu.VMEM((cols, pos), logits.dtype),
@@ -316,12 +324,20 @@
                 pltpu.SemaphoreType.DMA,
                 pltpu.SemaphoreType.DMA,
                 pltpu.SemaphoreType.DMA,
+                pltpu.SemaphoreType.REGULAR,
             ],
             compiler_params=pltpu.CompilerParams(collective_id=0, has_side_effects=True),
         )(
             logits.T, child_ids.T, leaf_counts.T,
             leaf_valid.reshape(1, pos), leaf_temp.reshape(1, pos), leaf_owner.reshape(1, pos),
         )
+        gradient, row_loss, mean_loss = pl.pallas_call(
+            leave,
+            out_shape=[jax.ShapeDtypeStruct(value.shape, value.dtype) for value in results],
+            in_specs=[vmem] * 3,
+            out_specs=[anywhere] * 3,
+            scratch_shapes=[pltpu.SemaphoreType.DMA((3,))],
+        )(*(pltpu.with_memory_space_constraint(value, pltpu.VMEM) for value in results))
         return gradient.T, row_loss.reshape(pos), mean_loss[0, 0]
 
     return jax.shard_map(

time: 38.5 us -> 36.1 us (0.938)
  local copies, waits for them, and re-layouts: 1.99 us -> 0 us
  between operations: 1.81 us -> 0.64 us
  Pallas kernels: 34.5 us -> 35.3 us
    unnamed x2 -> x0, local copies, waits for them, and re-layouts: 1.99 us -> none
    pallas_call x0 -> x1, Pallas kernels: none -> 1.46 us  [body(): pl.pallas_call(leave, out_shape=[jax.ShapeDtypeStruct(value.shape, value....]
    pallas_call x1, Pallas kernels: 34.5 us -> 33.8 us  [body(): pl.pallas_call(functools.partial(kernel, groups, shards), out_shape=(pltp...]
where the time goes in v4:
time: 36.1 us; the launch traced here: 35.9 us
  Pallas kernels  35.3 us (98%)
  between operations  0.64 us (2%)
    pallas_call x1, Pallas kernels, body(): pl.pallas_call(functools.partial(kernel, groups, shards), out_shape=(pltp...  33.8 us
    pallas_call x1, Pallas kernels, body(): pl.pallas_call(leave, out_shape=[jax.ShapeDtypeStruct(value.shape, value....  1.46 us

profile of v4, /device:TPU:1, one launch (start us, length us, event | category | flops | bytes accessed | tf_op | source)
XLA Modules:
  0.0 35.9 jit_solution(15086190563804626263)
XLA Ops:
  0.6 33.8 %shard_map.85 = (bf16[4752,256]{1,0:T(8,128)(2,1)S(1)}, f32[1,256]{1,0:T(1,128)S(1)}, f32[1,128]{1,0:T(1,128)S(1)}) custom-call(bf16[4752,256]{1,0:T(8,128)(2,1)} %bitcast.10, s32[64,256]{1,0:T(8,128)} %bitcast.11, s32[64,256]{1,0:T(8,128)} %bitcast.12, s32[1,256]{1,0:T(1,128)} %bitcast.13, f32[1,256]{1,0:T(1,128)} %bitcast.14, s32[1,256]{1,0:T(1,128)} %bitcast.15), custom_call_target="tpu_custom_call" | custom-call | tf_op jit(solution)/shard_map/pallas_call | solution.py:298
  34.5 1.5 %shard_map.86 = (bf16[4752,256]{1,0:T(8,128)(2,1)}, f32[1,256]{1,0:T(1,128)}, f32[1,128]{1,0:T(1,128)}) custom-call(bf16[4752,256]{1,0:T(8,128)(2,1)S(1)} %get-tuple-element.9.refs_0_, f32[1,256]{1,0:T(1,128)S(1)} %get-tuple-element.10.refs_1_, f32[1,128]{1,0:T(1,128)S(1)} %get-tuple-element.11.refs_2_), custom_call_target="tpu_custom_call" | custom-call | tf_op jit(solution)/shard_map/pallas_call | solution.py:334

commit v5 on v4

--- a/solution.py
+++ b/solution.py
@@ -52,14 +52,20 @@
 
 def kernel(
     groups, shards,
-    x_hbm, ids_ref, count_ref, valid_ref, temp_ref, owner_ref,
+    x_hbm, ids_hbm, count_hbm, valid_hbm, temp_hbm, owner_hbm,
     gout, loss_ref, mean_ref,
+    ids_ref, count_ref, valid_ref, temp_ref, owner_ref,
     xs, es, dense, turned_x, outbuf, inbuf, head_rows, rest_rows, at_ids, parts,
     stat_send, stat_buf, mean_send, mean_buf,
-    x_sem, send_sem, route_sem, stat_sem, mean_sem, hello_sem,
+    in_sem, x_sem, send_sem, route_sem, stat_sem, mean_sem, hello_sem,
 ):
     cols, pos = x_hbm.shape
     child = ids_ref.shape[0]
+    sources = (count_hbm, valid_hbm, temp_hbm, owner_hbm, ids_hbm)
+    kept = (count_ref, valid_ref, temp_ref, owner_ref, ids_ref)
+    loads = [pltpu.make_async_copy(source, ref, in_sem.at[k]) for k, (source, ref) in enumerate(zip(sources, kept))]
+    for load in loads:
+        load.start()
     cap = pos // groups
     my_dp = lax.axis_index("dp")
     my_t = lax.axis_index("tensor")
@@ -78,6 +84,9 @@
         pl.semaphore_signal(barrier, inc=1, device_id={"tensor": peer_of(my_t, k, shards)}, device_id_type=MESH)
     for k in offsets(groups):
         pl.semaphore_signal(barrier, inc=1, device_id={"dp": peer_of(my_dp, k, groups)}, device_id_type=MESH)
+
+    for load in loads:
+        load.wait()
 
     powered = jnp.exp(jnp.log(count_ref[...].astype(F32)) * temp_ref[...])
     weights = jnp.where(iota((child, pos), 0) < valid_ref[...], powered, 0.0)
@@ -109,30 +118,15 @@
     rest_rows[...] = lax.bitwise_and(local, WIDE - 1).astype(F32)
 
     x_copy.wait()
-    steps = cols // CHUNK
-
-    def part(g):
-        return pl.ds(pl.multiple_of(g * CHUNK, CHUNK), CHUNK)
-
-    def fold(value):
-        return value.reshape(CHUNK // 8, 8, pos)
-
-    def peaks(values):
-        return jnp.max(values.reshape(CHUNK // 16, 16, pos), axis=0)
-
-    def tops(g, top):
-        return jnp.maximum(top, peaks(xs[part(g), :]))
-
-    top = lax.fori_loop(1, steps, tops, peaks(xs[0:CHUNK, :]))
-    top = jnp.max(top.astype(F32), axis=0, keepdims=True)
-
-    def sums(g, total):
-        powers = jnp.exp(xs[part(g), :].astype(F32) - top)
-        es[part(g), :] = powers
-        return total + jnp.sum(fold(powers), axis=0)
-
-    total = lax.fori_loop(0, steps, sums, jnp.zeros((8, pos), F32))
-    own_sum = jnp.sum(total, axis=0, keepdims=True)
+    xs[cols:, :] = jnp.zeros((xs.shape[0] - cols, pos), xs.dtype)
+
+    def turn(h):
+        at = h * WIDE if isinstance(h, int) else pl.multiple_of(h * WIDE, WIDE)
+        tile = jnp.transpose(xs[pl.ds(at, WIDE), :]).astype(F32)
+        for c in range(WIDE // LANES):
+            turned_x[c, pl.ds(h, pos, stride=HEADS), :] = tile[:, c * LANES : (c + 1) * LANES]
+
+    repeat(heads, 3, turn)
 
     pl.semaphore_wait(barrier, groups - 1 + len(near))
 
@@ -157,15 +151,30 @@
         pl.semaphore_signal(hello_sem, inc=1, device_id={"tensor": peer_of(my_t, k, shards)}, device_id_type=MESH)
     inbuf[pl.ds(my_dp, 1)] = outbuf[pl.ds(my_dp, 1)]
 
-    xs[cols:, :] = jnp.zeros((xs.shape[0] - cols, pos), xs.dtype)
-
-    def turn(h):
-        at = h * WIDE if isinstance(h, int) else pl.multiple_of(h * WIDE, WIDE)
-        tile = jnp.transpose(xs[pl.ds(at, WIDE), :]).astype(F32)
-        for c in range(WIDE // LANES):
-            turned_x[c, pl.ds(h, pos, stride=HEADS), :] = tile[:, c * LANES : (c + 1) * LANES]
-
-    repeat(heads, 3, turn)
+    steps = cols // CHUNK
+
+    def part(g):
+        return pl.ds(pl.multiple_of(g * CHUNK, CHUNK), CHUNK)
+
+    def fold(value):
+        return value.reshape(CHUNK // 8, 8, pos)
+
+    def peaks(values):
+        return jnp.max(values.reshape(CHUNK // 16, 16, pos), axis=0)
+
+    def tops(g, top):
+        return jnp.maximum(top, peaks(xs[part(g), :]))
+
+    top = lax.fori_loop(1, steps, tops, peaks(xs[0:CHUNK, :]))
+    top = jnp.max(top.astype(F32), axis=0, keepdims=True)
+
+    def sums(g, total):
+        powers = jnp.exp(xs[part(g), :].astype(F32) - top)
+        es[part(g), :] = powers
+        return total + jnp.sum(fold(powers), axis=0)
+
+    total = lax.fori_loop(0, steps, sums, jnp.zeros((8, pos), F32))
+    own_sum = jnp.sum(total, axis=0, keepdims=True)
 
     spread_rows = iota((WIDE, LANES), 0).astype(F32).astype(BF16)
     one = jnp.ones((WIDE, LANES), BF16)
@@ -302,9 +311,14 @@
                 pltpu.VMEM((1, pos), F32),
                 pltpu.VMEM((1, LANES), F32),
             ),
-            in_specs=[anywhere] + [vmem] * 5,
+            in_specs=[anywhere] * 6,
             out_specs=(vmem, vmem, vmem),
             scratch_shapes=[
+                pltpu.VMEM((child, pos), jnp.int32),
+                pltpu.VMEM((child, pos), jnp.int32),
+                pltpu.VMEM((1, pos), jnp.int32),
+                pltpu.VMEM((1, pos), F32),
+                pltpu.VMEM((1, pos), jnp.int32),
                 pltpu.VMEM((padded, pos), logits.dtype),
                 pltpu.VMEM((cols, pos), F32),
                 pltpu.VMEM((WIDE // LANES, pos * HEADS, LANES), F32),
@@ -319,6 +333,7 @@
                 pltpu.VMEM((shards, 3, pos), F32),
                 pltpu.VMEM((1, LANES), F32),
                 pltpu.VMEM((groups, 1, LANES), F32),
+                pltpu.SemaphoreType.DMA((5,)),
                 pltpu.SemaphoreType.DMA,
                 pltpu.SemaphoreType.DMA((3,)),
                 pltpu.SemaphoreType.DMA,

time: 36.1 us -> 35.3 us (0.978)
  Pallas kernels: 35.3 us -> 34.5 us
    pallas_call x1, Pallas kernels: 33.8 us -> 33 us  [body(): pl.pallas_call(functools.partial(kernel, groups, shards), out_shape=(pltp...]
where the time goes in v5:
time: 35.3 us; the launch traced here: 35.1 us
  Pallas kernels  34.5 us (98%)
  between operations  0.64 us (2%)
    pallas_call x1, Pallas kernels, body(): pl.pallas_call(functools.partial(kernel, groups, shards), out_shape=(pltp...  33 us
    pallas_call x1, Pallas kernels, body(): pl.pallas_call(leave, out_shape=[jax.ShapeDtypeStruct(value.shape, value....  1.46 us

profile of v5, /device:TPU:1, one launch (start us, length us, event | category | flops | bytes accessed | tf_op | source)
XLA Modules:
  0.0 35.1 jit_solution(6158032917612598714)
XLA Ops:
  0.6 33.0 %shard_map.85 = (bf16[4752,256]{1,0:T(8,128)(2,1)S(1)}, f32[1,256]{1,0:T(1,128)S(1)}, f32[1,128]{1,0:T(1,128)S(1)}) custom-call(bf16[4752,256]{1,0:T(8,128)(2,1)} %bitcast.10, s32[64,256]{1,0:T(8,128)} %bitcast.11, s32[64,256]{1,0:T(8,128)} %bitcast.12, s32[1,256]{1,0:T(1,128)} %bitcast.13, f32[1,256]{1,0:T(1,128)} %bitcast.14, s32[1,256]{1,0:T(1,128)} %bitcast.15), custom_call_target="tpu_custom_call" | custom-call | tf_op jit(solution)/shard_map/pallas_call | solution.py:307
  33.6 1.5 %shard_map.86 = (bf16[4752,256]{1,0:T(8,128)(2,1)}, f32[1,256]{1,0:T(1,128)}, f32[1,128]{1,0:T(1,128)}) custom-call(bf16[4752,256]{1,0:T(8,128)(2,1)S(1)} %get-tuple-element.9.refs_0_, f32[1,256]{1,0:T(1,128)S(1)} %get-tuple-element.10.refs_1_, f32[1,128]{1,0:T(1,128)S(1)} %get-tuple-element.11.refs_2_), custom_call_target="tpu_custom_call" | custom-call | tf_op jit(solution)/shard_map/pallas_call | solution.py:349
